TPU v7x, 256 devices: a whole 4x4x8 slice. The times are simulated.
256 devices in a mesh: dp: 8 (over x, core), expert: 32 (over z, y).
Axes of the slice: x: 4, y: 4, z: 8, core: 2. Of those that a mesh axis runs over, the one named last changes fastest.
Arguments:
- tokens: bfloat16 [2048, 6144], P('dp', 'expert'), may hold values from -6 to 6
- cotangent: bfloat16 [2048, 6144], P('dp', 'expert'), may hold values from -6 to 6
- expert_choice: int32 [2048, 2], P('dp'), may hold values from 0 to 7, all different within a row; in each aligned block of 256 rows (0 to 255, 256 to 511, ...) at most 80 rows name the same one
- gate_values: bfloat16 [2048, 2], P('dp'), may hold values from 0.099609375 to 1
- gate_weight: bfloat16 [8, 6144, 8192], P('dp', None, 'expert'), may hold values from -0.078125 to 0.078125
- up_weight: bfloat16 [8, 6144, 8192], P('dp', None, 'expert'), may hold values from -0.078125 to 0.078125
- down_weight: bfloat16 [8, 8192, 6144], P('dp', 'expert'), may hold values from -0.0625 to 0.0625
- shrinker: bfloat16 [8, 32, 6144], P('dp'), may hold values from -0.078125 to 0.078125
- widener: bfloat16 [8, 2, 16, 8192], P('dp', None, None, 'expert'), may hold values from -0.375 to 0.375
- squeezer: bfloat16 [8, 16, 8192], P('dp', None, 'expert'), may hold values from -0.0625 to 0.0625
- spreader: bfloat16 [8, 16, 6144], P('dp'), may hold values from -0.375 to 0.375
Outputs:
- token_grad: bfloat16 [2048, 6144], P('dp', 'expert')
- gate_grad: float32 [2048, 2], P('dp')
- shrinker_grad: float32 [8, 32, 6144], P('dp')
- widener_grad: float32 [8, 2, 16, 8192], P('dp', None, None, 'expert')
- squeezer_grad: float32 [8, 16, 8192], P('dp', None, 'expert')
- spreader_grad: float32 [8, 16, 6144], P('dp')
Inputs may be any that keep to these rules, and one draw needn't show every extreme that they name: `expert_choice`: each row names 2 different experts. Among the 256 tokens of one index of dp no expert is chosen more than 80 times, and some expert is chosen exactly 80 times by the tokens of some or all indices of dp.
All inputs are finite; a program needn't handle non-finite values.
Results may differ from a plain program's by a relative error of at most 0.02.
Values may be sent and summed in bfloat16 or wider, within the bound.
No kernel may reach another device: no remote copies, remote signals or barrier semaphores. Data moves between devices by JAX's collectives and lax.ppermute only.
A program may use at most 128 MiB of HBM per device.

v0:
```python
import jax
import jax.numpy as jnp
from jax import lax
from jax.sharding import PartitionSpec as P

adapter_scale = 2.0


def product(pattern, operand_a, operand_b):
    return jnp.einsum(pattern, operand_a, operand_b, preferred_element_type=jnp.float32)


def silu_pair(gate_pre):
    logistic = jax.nn.sigmoid(gate_pre)
    return (gate_pre * logistic, logistic * (1.0 + gate_pre * (1.0 - logistic)))


def full_rows(gathered, capacity, part_width):
    n_groups = gathered.shape[0]
    n_sources = gathered.shape[1]
    ordered = gathered.reshape(n_groups, n_sources, capacity, part_width).transpose(1, 2, 0, 3)
    return ordered.reshape(n_sources * capacity, n_groups * part_width)


def local(
    tokens,
    cotangent,
    expert_choice,
    gate_values,
    gate_weight,
    up_weight,
    down_weight,
    shrinker,
    widener,
    squeezer,
    spreader,
):
    tok_rows, part_width = tokens.shape
    top_k = expert_choice.shape[1]
    low_rank = spreader.shape[1]
    n_groups = lax.axis_size("expert")
    n_experts = lax.axis_size("dp")
    capacity = tok_rows * top_k * 5 // (4 * n_experts)
    own_rows = n_experts * capacity
    flat_choice = expert_choice.reshape(-1)
    onehot = (flat_choice[:, None] == jnp.arange(n_experts, dtype=jnp.int32)[None, :]).astype(
        jnp.int32
    )
    before = jnp.cumsum(onehot, axis=0) - onehot
    slot_index = jnp.sum(before * onehot, axis=1)
    target = flat_choice * capacity + slot_index
    placing = target[None, :] == jnp.arange(own_rows, dtype=jnp.int32)[:, None]
    stacked = jnp.repeat(jnp.concatenate([tokens, cotangent], axis=1), top_k, axis=0)
    placed = jnp.dot(
        placing.astype(jnp.bfloat16), stacked, preferred_element_type=jnp.float32
    ).astype(jnp.bfloat16)
    send_x = placed[:, :part_width].reshape(n_experts, capacity * part_width)
    send_dy = placed[:, part_width:].reshape(n_experts, capacity * part_width)
    gate_flat = gate_values.reshape(-1).astype(jnp.float32)
    send_gate = (
        jnp.sum(jnp.where(placing, gate_flat[None, :], 0.0), axis=1)
        .astype(jnp.bfloat16)
        .reshape(n_experts, capacity)
    )
    recv_x, recv_dy, recv_gate = (
        lax.all_to_all(send_x, "dp", split_axis=0, concat_axis=0, tiled=True),
        lax.all_to_all(send_dy, "dp", split_axis=0, concat_axis=0, tiled=True),
        lax.all_to_all(send_gate, "dp", split_axis=0, concat_axis=0, tiled=True),
    )
    gate_rows = recv_gate.reshape(-1).astype(jnp.float32)
    gathered_x, gathered_dy = (
        lax.all_gather(recv_x[None], "expert", axis=0, tiled=True),
        lax.all_gather(recv_dy[None], "expert", axis=0, tiled=True),
    )
    rows_dy = full_rows(gathered_dy, capacity, part_width)
    rows_x = full_rows(gathered_x, capacity, part_width)
    shrink_local = shrinker[0]
    widen_local = widener[0]
    squeeze_local = squeezer[0]
    spread_local = spreader[0]
    lowrank_in = product("nd,rd->nr", rows_x, shrink_local).astype(jnp.bfloat16)
    gate_pre = jnp.dot(
        rows_x, gate_weight[0], preferred_element_type=jnp.float32
    ) + adapter_scale * jnp.dot(
        lowrank_in[:, :low_rank], widen_local[0], preferred_element_type=jnp.float32
    )
    up_pre = jnp.dot(
        rows_x, up_weight[0], preferred_element_type=jnp.float32
    ) + adapter_scale * jnp.dot(
        lowrank_in[:, low_rank:], widen_local[1], preferred_element_type=jnp.float32
    )
    silu_gate, silu_slope = silu_pair(gate_pre)
    activation = (silu_gate * up_pre).astype(jnp.bfloat16)
    out_part = product("rf,nf->rn", squeeze_local, activation)
    out_low = lax.psum(out_part.astype(jnp.bfloat16), "expert").astype(jnp.float32)
    back_down = product("nd,fd->nf", rows_dy, down_weight[0])
    back_low = product("rd,nd->rn", spread_local, rows_dy)
    gate_part = jnp.sum(activation.astype(jnp.float32) * back_down, axis=1)
    scaled_low = (back_low * gate_rows[None, :]).astype(jnp.bfloat16)
    act_delta = gate_rows[:, None] * back_down + adapter_scale * product(
        "rn,rf->nf", scaled_low, squeeze_local
    )
    gate_delta = (act_delta * up_pre * silu_slope).astype(jnp.bfloat16)
    up_delta = (act_delta * silu_gate).astype(jnp.bfloat16)
    back_part = jnp.concatenate(
        [
            product("rf,nf->rn", widen_local[0], gate_delta),
            product("rf,nf->rn", widen_local[1], up_delta),
        ],
        axis=0,
    )
    back_sum, gate_sum = (
        lax.psum(back_part.astype(jnp.bfloat16), "expert").astype(jnp.float32),
        lax.psum(gate_part.astype(jnp.bfloat16), "expert").astype(jnp.float32),
    )
    low_out = out_low.astype(jnp.bfloat16)
    gate_dots = gate_sum + adapter_scale * jnp.sum(low_out.astype(jnp.float32) * back_low, axis=0)
    back_in = back_sum.astype(jnp.bfloat16)
    gate_blocks = gate_weight[0].reshape(n_groups, part_width, gate_weight.shape[2])
    up_blocks = up_weight[0].reshape(n_groups, part_width, up_weight.shape[2])
    term = product("nf,kdf->knd", gate_delta, gate_blocks) + product(
        "nf,kdf->knd", up_delta, up_blocks
    )
    token_part = (
        lax.psum_scatter(
            term.reshape(1 * lax.axis_size("expert"), own_rows * part_width).astype(jnp.bfloat16),
            "expert",
            scatter_dimension=0,
            tiled=True,
        )
        .astype(jnp.float32)
        .reshape(own_rows, part_width)
    )
    shrink_cols = lax.dynamic_slice_in_dim(
        shrink_local, lax.axis_index("expert") * part_width, part_width, 1
    )
    token_part = token_part + adapter_scale * product("rn,rd->nd", back_in, shrink_cols)
    token_back, gate_back = (
        lax.all_to_all(
            token_part.reshape(n_experts, capacity * part_width).astype(jnp.bfloat16),
            "dp",
            split_axis=0,
            concat_axis=0,
            tiled=True,
        ).astype(jnp.float32),
        lax.all_to_all(
            gate_dots.reshape(n_experts, capacity).astype(jnp.bfloat16),
            "dp",
            split_axis=0,
            concat_axis=0,
            tiled=True,
        ).astype(jnp.float32),
    )
    picked = jnp.take(token_back.reshape(own_rows, part_width), target, axis=0)
    token_grad = jnp.sum(picked.reshape(tok_rows, top_k, part_width), axis=1).astype(jnp.bfloat16)
    gate_grad = jnp.take(gate_back.reshape(own_rows), target).reshape(tok_rows, top_k)
    shrinker_grad = adapter_scale * product("rn,nd->rd", back_in, rows_x)
    widener_grad = adapter_scale * jnp.stack(
        [
            product("nr,nf->rf", lowrank_in[:, :low_rank], gate_delta),
            product("nr,nf->rf", lowrank_in[:, low_rank:], up_delta),
        ]
    )
    squeezer_grad = adapter_scale * product("rn,nf->rf", scaled_low, activation)
    weighted_low = (out_low * gate_rows[None, :]).astype(jnp.bfloat16)
    spreader_grad = adapter_scale * product("rn,nd->rd", weighted_low, rows_dy)
    return (
        token_grad,
        gate_grad,
        shrinker_grad[None],
        widener_grad[None],
        squeezer_grad[None],
        spreader_grad[None],
    )


def solution(mesh):
    placed = (
        P("dp", "expert"),
        P("dp", "expert"),
        P("dp", None),
        P("dp", None),
        P("dp", None, "expert"),
        P("dp", None, "expert"),
        P("dp", "expert", None),
        P("dp", None, None),
        P("dp", None, None, "expert"),
        P("dp", None, "expert"),
        P("dp", None, None),
    )
    return jax.shard_map(
        local,
        mesh=mesh,
        in_specs=placed,
        out_specs=(
            P("dp", "expert"),
            P("dp", None),
            P("dp", None, None),
            P("dp", None, None, "expert"),
            P("dp", None, "expert"),
            P("dp", None, None),
        ),
        check_vma=False,
    )
```

profile of v0, /device:TPU:1, one launch (start us, length us, event | category | flops | bytes accessed | tf_op | source)
XLA Modules:
  0.0 594.0 jit_solution(10980135344185267276)
XLA Ops:
  21.3 3.0 reduce.16
  25.2 12.8 %all_to_all.38 = bf16[8,2,7680]{2,1,0:T(2,128)(2,1)S(1)} all-to-all(bf16[8,2,7680]{2,1,0:T(2,128)(2,1)} %reshape.290), channel_id=1, replica_groups=mesh['dp'=8,'expert'=32] {'dp'}, dimensions={0} | all-to-all | bytes 491520 | tf_op jit(solution)/shard_map/all_to_all | solution.py:67
  44.8 3.0 reduce.17
  48.7 10.7 %all_to_all.39 = bf16[8,2,7680]{2,1,0:T(2,128)(2,1)S(1)} all-to-all(bf16[8,2,7680]{2,1,0:T(2,128)(2,1)} %reshape.288), channel_id=1, replica_groups=mesh['dp'=8,'expert'=32] {'dp'}, dimensions={0} | all-to-all | bytes 491520 | tf_op jit(solution)/shard_map/all_to_all | solution.py:66
  62.7 8.1 %all_to_all.40 = bf16[8,1,80]{2,1,0:T(2,128)(2,1)S(1)} all-to-all(bf16[8,1,80]{2,1,0:T(2,128)(2,1)S(1)} %convert_element_type.180), channel_id=1, replica_groups=mesh['dp'=8,'expert'=32] {'dp'}, dimensions={0} | all-to-all | bytes 2560 | tf_op jit(solution)/shard_map/all_to_all | solution.py:68
  70.9 65.3 %all-gather.5.cloned.1.call-done = bf16[256,1,15360]{2,0,1:T(8,128)(2,1)} async-done(((bf16[8,1,15360]{2,0,1:T(8,128)(2,1)}), bf16[256,1,15360]{2,0,1:T(8,128)(2,1)}) %all-gather.5.cloned.1.call-update) | async-done | bytes 7864336 | tf_op jit(solution)/shard_map/all_gather | solution.py:73
  136.2 18.1 %reshape.231 = bf16[32,8,80,192]{3,2,1,0:T(8,128)(2,1)} reshape(bf16[256,1,15360]{2,0,1:T(8,128)(2,1)} %all-gather.5.cloned.1.call-done) | data formatting | bytes 15728640 | tf_op jit(solution)/shard_map/reshape | solution.py:21
  154.3 13.9 %copy.93 = bf16[8,80,32,192]{3,2,1,0:T(8,128)(2,1)} copy(bf16[8,80,32,192]{3,1,0,2:T(8,128)(2,1)} %bitcast.103) | data formatting | bytes 15728640 | tf_op jit(solution)/shard_map/transpose | solution.py:21
  168.2 18.2 %reshape.232 = bf16[640,6144]{1,0:T(8,128)(2,1)} reshape(bf16[8,80,32,192]{3,2,1,0:T(8,128)(2,1)} %copy.93) | data formatting | bytes 15728640 | tf_op jit(solution)/shard_map/reshape | solution.py:22
  186.4 6.0 %convolution_bitcast_fusion = f32[16,640]{1,0:T(8,128)S(1)} fusion(bf16[640,6144]{1,0:T(8,128)(2,1)} %reshape.232, bf16[1,16,6144]{2,1,0:T(8,128)(2,1)S(1)} %copy-done.8), kind=kOutput, calls=%fused_computation.28 | convolution fusion | flops 125829120 | bytes 8101888 | tf_op jit(solution)/shard_map/rd,nd->rn/dot_general | solution.py:10
  192.4 5.4 fusion.7
  197.8 33.9 %all-gather.7.cloned.1.call-done = bf16[256,1,15360]{2,0,1:T(8,128)(2,1)} async-done(((bf16[8,1,15360]{2,0,1:T(8,128)(2,1)}), bf16[256,1,15360]{2,0,1:T(8,128)(2,1)}) %all-gather.7.cloned.1.call-update) | async-done | bytes 7864336 | tf_op jit(solution)/shard_map/all_gather | solution.py:72
  231.7 18.3 %reshape.233 = bf16[32,8,80,192]{3,2,1,0:T(8,128)(2,1)} reshape(bf16[256,1,15360]{2,0,1:T(8,128)(2,1)} %all-gather.7.cloned.1.call-done) | data formatting | bytes 15728640 | tf_op jit(solution)/shard_map/reshape | solution.py:21
  249.9 13.8 %copy.98 = bf16[8,80,32,192]{3,2,1,0:T(8,128)(2,1)} copy(bf16[8,80,32,192]{3,1,0,2:T(8,128)(2,1)} %bitcast.104) | data formatting | bytes 15728640 | tf_op jit(solution)/shard_map/transpose | solution.py:21
  263.8 18.5 %reshape.234 = bf16[640,6144]{1,0:T(8,128)(2,1)} reshape(bf16[8,80,32,192]{3,2,1,0:T(8,128)(2,1)} %copy.98) | data formatting | bytes 15728640 | tf_op jit(solution)/shard_map/reshape | solution.py:22
  282.3 5.8 convolution_convert_fusion
  291.1 2.9 fusion.5
  295.9 6.8 %fusion.25 = f32[640,32,192]{0,2,1:T(8,128)} fusion(bf16[32,192,256]{2,1,0:T(8,128)(2,1)S(1)} %bitcast.102, bf16[640,256]{0,1:T(8,128)(2,1)S(1)} %get-tuple-element.37), kind=kOutput, calls=%fused_computation.53 | convolution fusion | flops 2013265920 | bytes 19202048 | tf_op jit(solution)/shard_map/nf,kdf->knd/dot_general | solution.py:10
  302.7 8.8 %fusion.2 = bf16[32,640,192]{1,2,0:T(8,128)(2,1)} fusion(f32[640,32,192]{0,2,1:T(8,128)} %fusion.25, bf16[32,192,256]{2,1,0:T(8,128)(2,1)S(1)} %bitcast.105, bf16[640,256]{0,1:T(8,128)(2,1)S(1)} %get-tuple-element.38), kind=kOutput, calls=%fused_computation.7 | convolution fusion | flops 2021130240 | bytes 27066368 | tf_op jit(solution)/shard_map/nf,kdf->knd/dot_general | solution.py:10
  311.6 13.7 %copy.101 = bf16[32,640,192]{2,1,0:T(8,128)(2,1)} copy(bf16[32,640,192]{1,2,0:T(8,128)(2,1)} %fusion.2) | data formatting | bytes 15728640 | tf_op jit(solution)/shard_map/convert_element_type | solution.py:126
  325.3 15.6 %convert_element_type.158 = bf16[32,122880]{1,0:T(8,128)(2,1)} reshape(bf16[32,640,192]{2,1,0:T(8,128)(2,1)} %copy.101) | data formatting | bytes 15728640 | tf_op jit(solution)/shard_map/convert_element_type | solution.py:126
  345.9 114.8 %all-reduce.1 = (bf16[32,640]{1,0:T(8,128)(2,1)S(1)}, bf16[16,640]{1,0:T(8,128)(2,1)S(1)}, bf16[640]{0:T(1024)(128)(2,1)S(1)}) all-reduce(bf16[32,640]{1,0:T(8,128)(2,1)S(1)} %pad_maximum_fusion.1, bf16[16,640]{1,0:T(8,128)(2,1)S(1)} %fusion.18, bf16[640]{0:T(1024)(128)(2,1)S(1)} %get-tuple-element.35), channel_id=1, replica_groups=mesh['dp'=8,'expert'=32] {'expert'}, use_global_device_ids=true, to_apply=%region_5.6 | all-reduce | flops 31360 | bytes 125440 | tf_op jit(solution)/shard_map/psum | solution.py:113
  461.4 32.7 %all-to-all-start.4 = ((bf16[8,1,80]{2,1,0:T(2,128)(2,1)}), bf16[8,1,80]{2,1,0:T(2,128)(2,1)S(1)}, u32[]{:S(2)}, u32[]{:S(2)}) async-start(bf16[8,1,80]{2,1,0:T(2,128)(2,1)} %convert_element_type.182), calls=%async_computation.4 | async-start | bytes 8192 | tf_op jit(solution)/shard_map/all_to_all | solution.py:146
  498.3 5.3 fusion.1
  503.5 5.7 fusion
  513.0 30.8 %all-reduce.4.cloned.1.call-done = bf16[32,122880]{1,0:T(8,128)(2,1)} async-done(((bf16[32,122880]{1,0:T(8,128)(2,1)}), bf16[32,122880]{1,0:T(8,128)(2,1)}) %all-reduce.4.cloned.1.call-update) | async-done | bytes 7864336
  543.8 4.4 fusion.22
  556.8 3.0 reduce.18
  560.7 5.4 all-to-all-start.3
  569.4 3.0 all-to-all-done.3
  573.3 3.2 convert_reduce_fusion
  578.6 3.3 gather_fusion
  (106 shorter events, 65.4 us)
Async XLA Ops:
  7.2 280.9 %copy-start = (bf16[1,6144,256]{2,1,0:T(8,128)(2,1)S(1)}, bf16[1,6144,256]{2,1,0:T(8,128)(2,1)}, u32[]{:S(2)}) copy-start(bf16[1,6144,256]{2,1,0:T(8,128)(2,1)} %param.15) | copy-start | bytes 9437188
  7.2 54.9 %copy-start.12 = (bf16[256,2]{0,1:T(2,128)(2,1)S(1)}, bf16[256,2]{0,1:T(2,128)(2,1)}, u32[]{:S(2)}) copy-start(bf16[256,2]{0,1:T(2,128)(2,1)} %param.14) | copy-start | bytes 3076
  7.2 129.0 %all-gather.5.cloned.1.call-start = ((), (), s32[]{:S(2)}) async-start(), calls=%async_computation.5 | async-start | bytes 8110080 | tf_op jit(solution)/shard_map/all_gather | solution.py:73
  40.8 190.9 %all-gather.7.cloned.1.call-start = ((), (), s32[]{:S(2)}) async-start(), calls=%async_computation.6 | async-start | bytes 8110080 | tf_op jit(solution)/shard_map/all_gather | solution.py:72
  62.1 481.8 %all-reduce.4.cloned.1.call-start = ((), (), s32[]{:S(2)}) async-start(), calls=%async_computation.7 | async-start | bytes 15728640
  168.2 18.2 %copy-start.8 = (bf16[1,16,6144]{2,1,0:T(8,128)(2,1)S(1)}, bf16[1,16,6144]{2,1,0:T(8,128)(2,1)}, u32[]{:S(2)}) copy-start(bf16[1,16,6144]{2,1,0:T(8,128)(2,1)} %param.21) | copy-start | bytes 589828
  186.4 6.0 %copy-start.1 = (bf16[640,6144]{1,0:T(8,128)(2,1)S(1)}, bf16[640,6144]{1,0:T(8,128)(2,1)}, u32[]{:S(2)}) copy-start(bf16[640,6144]{1,0:T(8,128)(2,1)} %reshape.232) | copy-start | bytes 23592964
  282.3 5.8 copy-start.2
  288.1 2.9 copy-start.3
  291.0 3.0 copy-start.10
  291.0 3.3 copy-start.6
  291.0 3.3 copy-start.11
  295.9 6.8 %copy-start.5 = (bf16[640,256]{0,1:T(8,128)(2,1)}, bf16[640,256]{0,1:T(8,128)(2,1)S(1)}, u32[]{:S(2)}) copy-start(bf16[640,256]{0,1:T(8,128)(2,1)S(1)} %get-tuple-element.37) | copy-start | bytes 983044
  295.9 6.8 %copy-start.4 = (bf16[640,256]{0,1:T(8,128)(2,1)}, bf16[640,256]{0,1:T(8,128)(2,1)S(1)}, u32[]{:S(2)}) copy-start(bf16[640,256]{0,1:T(8,128)(2,1)S(1)} %get-tuple-element.38) | copy-start | bytes 983044
  340.8 1.0 copy-start.13
  460.7 48.6 %copy-start.7 = (bf16[32,640]{1,0:T(8,128)(2,1)}, bf16[32,640]{1,0:T(8,128)(2,1)S(1)}, u32[]{:S(2)}) copy-start(bf16[32,640]{1,0:T(8,128)(2,1)S(1)} %get-tuple-element.30) | copy-start | bytes 122884
  461.4 48.5 %all-to-all-start.4 = ((bf16[8,1,80]{2,1,0:T(2,128)(2,1)}), bf16[8,1,80]{2,1,0:T(2,128)(2,1)S(1)}, u32[]{:S(2)}, u32[]{:S(2)}) async-start(bf16[8,1,80]{2,1,0:T(2,128)(2,1)} %convert_element_type.182), calls=%async_computation.4 | async-start | bytes 8192 | tf_op jit(solution)/shard_map/all_to_all | solution.py:146
  560.7 11.7 %all-to-all-start.3 = ((bf16[8,2,7680]{2,1,0:T(2,128)(2,1)}), bf16[8,2,7680]{2,1,0:T(2,128)(2,1)S(1)}, u32[]{:S(2)}, u32[]{:S(2)}) async-start(bf16[8,2,7680]{2,1,0:T(2,128)(2,1)} %reshape.292), calls=%async_computation.3 | async-start | bytes 491520 | tf_op jit(solution)/shard_map/all_to_all | solution.py:139
  573.3 10.8 %copy-start.9 = (pred[256,2]{1,0:T(8,128)(4,1)S(1)}, pred[256,2]{1,0:T(8,128)(4,1)}, u32[]{:S(2)}) copy-start(pred[256,2]{1,0:T(8,128)(4,1)} %get-tuple-element.34) | copy-start | bytes 1540
Sparse Core Ops, SparseCore 0:
  40.9 95.2 all-gather.4
  139.3 92.2 all-gather.6
  341.0 202.8 all-reduce.3
where the time goes:
time: 603 us; the launch traced here: 594 us
  local copies, waits for them, and re-layouts  176 us (29%)
  blocking collectives  146 us (24%)
  waiting for transfers between devices  133 us (22%)
  matrix products  62 us (10%)
  starting transfers between devices  38.3 us (6%)
  other arithmetic  24 us (4%)
  between operations  14.3 us (2%)
    psum x1, blocking collectives, local(): lax.psum(back_part.astype(jnp.bfloat16), 'expert').astype(jnp.float32)  115 us
    all_gather x1, waiting for transfers between devices, local(): lax.all_gather(recv_dy[None], 'expert', axis=0, tiled=True)  65.3 us
    dot_general x15, matrix products, product(): jnp.einsum(pattern, operand_a, operand_b, preferred_element_type=jnp.floa...  53.1 us
    reshape x2, local copies, waits for them, and re-layouts, full_rows(): return ordered.reshape(n_sources * capacity, n_groups * part_width)  36.7 us
    reshape x2, local copies, waits for them, and re-layouts, full_rows(): gathered.reshape(n_groups, n_sources, capacity, part_width)  36.4 us
    all_gather x1, waiting for transfers between devices, local(): lax.all_gather(recv_x[None], 'expert', axis=0, tiled=True)  33.9 us
    all_to_all x1, starting transfers between devices, local(): lax.all_to_all(gate_dots.reshape(n_experts, capacity).astype(jnp.bfloat16...  32.7 us
    unnamed x4, waiting for transfers between devices  30.9 us
  transfers between devices with their start and end apart: 5, of which 4 were waited for; matrix products, arithmetic and copies ran while one was open for 17% of the time, Pallas kernels for 0%

commit v1 on v0

--- a/solution.py
+++ b/solution.py
@@ -110,7 +110,9 @@
         axis=0,
     )
     back_sum, gate_sum = (
-        lax.psum(back_part.astype(jnp.bfloat16), "expert").astype(jnp.float32),
+        jnp.sum(lax.all_gather(back_part.astype(jnp.bfloat16), "expert"), axis=0).astype(
+            jnp.float32
+        ),
         lax.psum(gate_part.astype(jnp.bfloat16), "expert").astype(jnp.float32),
     )
     low_out = out_low.astype(jnp.bfloat16)

time: 603 us -> 637 us (1.056)
  waiting for transfers between devices: 133 us -> 164 us
    unnamed x4 -> x5, waiting for transfers between devices: 30.9 us -> 64.2 us
  transfers between devices with their start and end apart: 5 -> 6, of which waited for: 4 -> 4; matrix products, arithmetic and copies ran while one was open for 17% -> 23% of each run, Pallas kernels for 0% -> 0%
where the time goes in v1:
time: 637 us; the launch traced here: 628 us
  local copies, waits for them, and re-layouts  176 us (28%)
  waiting for transfers between devices  164 us (26%)
  blocking collectives  146 us (23%)
  matrix products  62.2 us (10%)
  starting transfers between devices  38.3 us (6%)
  other arithmetic  26.9 us (4%)
  between operations  14.3 us (2%)
    psum x1, blocking collectives, local(): lax.psum(out_part.astype(jnp.bfloat16), 'expert').astype(jnp.float32)  115 us
    all_gather x1, waiting for transfers between devices, local(): lax.all_gather(recv_dy[None], 'expert', axis=0, tiled=True)  65.2 us
    unnamed x5, waiting for transfers between devices  64.2 us
    dot_general x15, matrix products, product(): jnp.einsum(pattern, operand_a, operand_b, preferred_element_type=jnp.floa...  53.4 us
    reshape x2, local copies, waits for them, and re-layouts, full_rows(): return ordered.reshape(n_sources * capacity, n_groups * part_width)  36.6 us
    reshape x2, local copies, waits for them, and re-layouts, full_rows(): gathered.reshape(n_groups, n_sources, capacity, part_width)  36.4 us
    all_gather x1, waiting for transfers between devices, local(): lax.all_gather(recv_x[None], 'expert', axis=0, tiled=True)  33.8 us
    all_to_all x1, starting transfers between devices, local(): lax.all_to_all(gate_dots.reshape(n_experts, capacity).astype(jnp.bfloat16...  33.1 us
  transfers between devices with their start and end apart: 6, of which 4 were waited for; matrix products, arithmetic and copies ran while one was open for 23% of the time, Pallas kernels for 0%

profile of v1, /device:TPU:1, one launch (start us, length us, event | category | flops | bytes accessed | tf_op | source)
XLA Modules:
  0.0 628.1 jit_solution(16361472242169310705)
XLA Ops:
  21.4 3.1 reduce.17
  25.4 12.8 %all_to_all.38 = bf16[8,2,7680]{2,1,0:T(2,128)(2,1)S(1)} all-to-all(bf16[8,2,7680]{2,1,0:T(2,128)(2,1)} %reshape.321), channel_id=1, replica_groups=mesh['dp'=8,'expert'=32] {'dp'}, dimensions={0} | all-to-all | bytes 491520 | tf_op jit(solution)/shard_map/all_to_all | solution.py:67
  44.9 3.1 reduce.18
  48.8 10.7 %all_to_all.39 = bf16[8,2,7680]{2,1,0:T(2,128)(2,1)S(1)} all-to-all(bf16[8,2,7680]{2,1,0:T(2,128)(2,1)} %reshape.319), channel_id=1, replica_groups=mesh['dp'=8,'expert'=32] {'dp'}, dimensions={0} | all-to-all | bytes 491520 | tf_op jit(solution)/shard_map/all_to_all | solution.py:66
  62.9 8.1 %all_to_all.40 = bf16[8,1,80]{2,1,0:T(2,128)(2,1)S(1)} all-to-all(bf16[8,1,80]{2,1,0:T(2,128)(2,1)S(1)} %convert_element_type.189), channel_id=1, replica_groups=mesh['dp'=8,'expert'=32] {'dp'}, dimensions={0} | all-to-all | bytes 2560 | tf_op jit(solution)/shard_map/all_to_all | solution.py:68
  71.1 65.2 %all-gather.8.cloned.1.call-done = bf16[256,1,15360]{2,0,1:T(8,128)(2,1)} async-done(((bf16[8,1,15360]{2,0,1:T(8,128)(2,1)}), bf16[256,1,15360]{2,0,1:T(8,128)(2,1)}) %all-gather.8.cloned.1.call-update) | async-done | bytes 7864336 | tf_op jit(solution)/shard_map/all_gather | solution.py:73
  136.3 18.1 %reshape.262 = bf16[32,8,80,192]{3,2,1,0:T(8,128)(2,1)} reshape(bf16[256,1,15360]{2,0,1:T(8,128)(2,1)} %all-gather.8.cloned.1.call-done) | data formatting | bytes 15728640 | tf_op jit(solution)/shard_map/reshape | solution.py:21
  154.4 13.9 %copy.93 = bf16[8,80,32,192]{3,2,1,0:T(8,128)(2,1)} copy(bf16[8,80,32,192]{3,1,0,2:T(8,128)(2,1)} %bitcast.107) | data formatting | bytes 15728640 | tf_op jit(solution)/shard_map/transpose | solution.py:21
  168.3 18.2 %reshape.263 = bf16[640,6144]{1,0:T(8,128)(2,1)} reshape(bf16[8,80,32,192]{3,2,1,0:T(8,128)(2,1)} %copy.93) | data formatting | bytes 15728640 | tf_op jit(solution)/shard_map/reshape | solution.py:22
  186.6 6.0 convolution_bitcast_fusion
  192.6 5.5 fusion.7
  198.0 33.8 %all-gather.10.cloned.1.call-done = bf16[256,1,15360]{2,0,1:T(8,128)(2,1)} async-done(((bf16[8,1,15360]{2,0,1:T(8,128)(2,1)}), bf16[256,1,15360]{2,0,1:T(8,128)(2,1)}) %all-gather.10.cloned.1.call-update) | async-done | bytes 7864336 | tf_op jit(solution)/shard_map/all_gather | solution.py:72
  231.8 18.3 %reshape.264 = bf16[32,8,80,192]{3,2,1,0:T(8,128)(2,1)} reshape(bf16[256,1,15360]{2,0,1:T(8,128)(2,1)} %all-gather.10.cloned.1.call-done) | data formatting | bytes 15728640 | tf_op jit(solution)/shard_map/reshape | solution.py:21
  250.1 13.8 %copy.98 = bf16[8,80,32,192]{3,2,1,0:T(8,128)(2,1)} copy(bf16[8,80,32,192]{3,1,0,2:T(8,128)(2,1)} %bitcast.108) | data formatting | bytes 15728640 | tf_op jit(solution)/shard_map/transpose | solution.py:21
  263.9 18.3 %reshape.265 = bf16[640,6144]{1,0:T(8,128)(2,1)} reshape(bf16[8,80,32,192]{3,2,1,0:T(8,128)(2,1)} %copy.98) | data formatting | bytes 15728640 | tf_op jit(solution)/shard_map/reshape | solution.py:22
  282.3 5.8 convolution_convert_fusion
  288.1 2.9 fusion.3
  291.0 2.9 fusion.5
  297.4 8.6 %fusion.25 = f32[640,32,192]{0,2,1:T(8,128)} fusion(bf16[32,192,256]{2,1,0:T(8,128)(2,1)S(1)} %bitcast.106, bf16[640,256]{0,1:T(8,128)(2,1)} %copy-done.7), kind=kOutput, calls=%fused_computation.53 | convolution fusion | flops 2013265920 | bytes 19202048 | tf_op jit(solution)/shard_map/nf,kdf->knd/dot_general | solution.py:10
  306.0 8.9 %fusion.2 = bf16[32,640,192]{1,2,0:T(8,128)(2,1)} fusion(f32[640,32,192]{0,2,1:T(8,128)} %fusion.25, bf16[32,192,256]{2,1,0:T(8,128)(2,1)S(1)} %bitcast.109, bf16[640,256]{0,1:T(8,128)(2,1)S(1)} %copy-done.6), kind=kOutput, calls=%fused_computation.7 | convolution fusion | flops 2021130240 | bytes 27066368 | tf_op jit(solution)/shard_map/nf,kdf->knd/dot_general | solution.py:10
  314.9 13.7 %copy.101 = bf16[32,640,192]{2,1,0:T(8,128)(2,1)} copy(bf16[32,640,192]{1,2,0:T(8,128)(2,1)} %fusion.2) | data formatting | bytes 15728640 | tf_op jit(solution)/shard_map/convert_element_type | solution.py:128
  328.6 15.5 %convert_element_type.167 = bf16[32,122880]{1,0:T(8,128)(2,1)} reshape(bf16[32,640,192]{2,1,0:T(8,128)(2,1)} %copy.101) | data formatting | bytes 15728640 | tf_op jit(solution)/shard_map/convert_element_type | solution.py:128
  347.7 114.7 %all-reduce.1 = (bf16[16,640]{1,0:T(8,128)(2,1)S(1)}, bf16[640]{0:T(1024)(128)(2,1)S(1)}) all-reduce(bf16[16,640]{1,0:T(8,128)(2,1)S(1)} %fusion.18, bf16[640]{0:T(1024)(128)(2,1)S(1)} %get-tuple-element.34), channel_id=1, replica_groups=mesh['dp'=8,'expert'=32] {'expert'}, use_global_device_ids=true, to_apply=%region_9.10 | all-reduce | flops 10880 | bytes 43520 | tf_op jit(solution)/shard_map/psum | solution.py:95
  463.1 33.1 %all-to-all-start.4 = ((bf16[8,1,80]{2,1,0:T(2,128)(2,1)}), bf16[8,1,80]{2,1,0:T(2,128)(2,1)S(1)}, u32[]{:S(2)}, u32[]{:S(2)}) async-start(bf16[8,1,80]{2,1,0:T(2,128)(2,1)} %convert_element_type.191), calls=%async_computation.4 | async-start | bytes 8192 | tf_op jit(solution)/shard_map/all_to_all | solution.py:148
  500.4 5.1 fusion.1
  514.0 64.1 %all-reduce.4.cloned.1.call-done = bf16[32,122880]{1,0:T(8,128)(2,1)} async-done(((bf16[32,122880]{1,0:T(8,128)(2,1)}), bf16[32,122880]{1,0:T(8,128)(2,1)}) %all-reduce.4.cloned.1.call-update) | async-done | bytes 7864336
  578.2 4.5 fusion.22
  591.2 3.1 reduce.19
  595.1 5.1 all-to-all-start.3
  600.2 5.6 fusion
  607.4 3.2 convert_reduce_fusion
  612.8 3.3 gather_fusion
  (110 shorter events, 65.0 us)
Async XLA Ops:
  7.2 280.9 %copy-start = (bf16[1,6144,256]{2,1,0:T(8,128)(2,1)S(1)}, bf16[1,6144,256]{2,1,0:T(8,128)(2,1)}, u32[]{:S(2)}) copy-start(bf16[1,6144,256]{2,1,0:T(8,128)(2,1)} %param.15) | copy-start | bytes 9437188
  7.2 55.1 %copy-start.12 = (bf16[256,2]{0,1:T(2,128)(2,1)S(1)}, bf16[256,2]{0,1:T(2,128)(2,1)}, u32[]{:S(2)}) copy-start(bf16[256,2]{0,1:T(2,128)(2,1)} %param.14) | copy-start | bytes 3076
  7.2 129.1 %all-gather.8.cloned.1.call-start = ((), (), s32[]{:S(2)}) async-start(), calls=%async_computation.6 | async-start | bytes 8110080 | tf_op jit(solution)/shard_map/all_gather | solution.py:73
  40.9 190.9 %all-gather.10.cloned.1.call-start = ((), (), s32[]{:S(2)}) async-start(), calls=%async_computation.7 | async-start | bytes 8110080 | tf_op jit(solution)/shard_map/all_gather | solution.py:72
  62.3 450.3 %all-gather.6.cloned.1.call-start = ((), (), s32[]{:S(2)}) async-start(), calls=%async_computation.5 | async-start | bytes 1351680 | tf_op jit(solution)/shard_map/all_gather | solution.py:113
  168.3 18.2 %copy-start.9 = (bf16[1,16,6144]{2,1,0:T(8,128)(2,1)S(1)}, bf16[1,16,6144]{2,1,0:T(8,128)(2,1)}, u32[]{:S(2)}) copy-start(bf16[1,16,6144]{2,1,0:T(8,128)(2,1)} %param.21) | copy-start | bytes 589828
  186.6 6.0 copy-start.2
  282.3 5.8 copy-start.1
  288.1 2.9 copy-start.3
  291.0 2.9 copy-start.10
  291.0 3.2 copy-start.8
  291.0 3.2 copy-start.11
  295.8 0.7 copy-start.5
  295.8 0.9 copy-start.7
  297.4 280.8 %all-reduce.4.cloned.1.call-start = ((), (), s32[]{:S(2)}) async-start(), calls=%async_computation.8 | async-start | bytes 15728640
  297.4 8.6 %copy-start.4 = (bf16[1,6144,256]{2,1,0:T(8,128)(2,1)S(1)}, bf16[1,6144,256]{2,1,0:T(8,128)(2,1)}, u32[]{:S(2)}) copy-start(bf16[1,6144,256]{2,1,0:T(8,128)(2,1)} %param.16) | copy-start | bytes 9437188
  297.4 8.6 %copy-start.6 = (bf16[640,256]{0,1:T(8,128)(2,1)S(1)}, bf16[640,256]{0,1:T(8,128)(2,1)}, u32[]{:S(2)}) copy-start(bf16[640,256]{0,1:T(8,128)(2,1)} %copy-done.5) | copy-start | bytes 983044
  344.0 1.9 copy-start.13
  463.1 43.0 %all-to-all-start.4 = ((bf16[8,1,80]{2,1,0:T(2,128)(2,1)}), bf16[8,1,80]{2,1,0:T(2,128)(2,1)S(1)}, u32[]{:S(2)}, u32[]{:S(2)}) async-start(bf16[8,1,80]{2,1,0:T(2,128)(2,1)} %convert_element_type.191), calls=%async_computation.4 | async-start | bytes 8192 | tf_op jit(solution)/shard_map/all_to_all | solution.py:148
  595.1 11.4 %all-to-all-start.3 = ((bf16[8,2,7680]{2,1,0:T(2,128)(2,1)}), bf16[8,2,7680]{2,1,0:T(2,128)(2,1)S(1)}, u32[]{:S(2)}, u32[]{:S(2)}) async-start(bf16[8,2,7680]{2,1,0:T(2,128)(2,1)} %reshape.323), calls=%async_computation.3 | async-start | bytes 491520 | tf_op jit(solution)/shard_map/all_to_all | solution.py:141
Sparse Core Ops, SparseCore 0:
  41.0 95.2 all-gather.7
  139.5 92.2 all-gather.9
  297.5 69.9 all-gather.5
  371.0 207.1 all-reduce.3
